TPU v7x, 512 devices: a whole 4x8x8 slice. The times are simulated.
512 devices in a mesh: elem: 128 (over z, x_lo, y), chan: 4 (over x_hi, core).
Axes of the slice: x: 4 (x_hi: 2, x_lo: 2; x = x_hi * 2 + x_lo), y: 8, z: 8, core: 2. Of those that a mesh axis runs over, the one named last changes fastest.
Arguments:
- voltages: bfloat16 [2, 16384, 19584], P(None, ('elem', 'chan')), may hold values from -6 to 6
- delays: int32 [16384], P(('elem', 'chan')), may hold values from 0 to 127
- prototype: bfloat16 [16, 1024], replicated, may hold values from -1.5 to 1.5
- subband_map: int32 [16], replicated, may hold values from 0 to 1023, as said below
- beam_weights: bfloat16 [512, 2, 16, 16384], P('elem', None, 'chan'), may hold values from -0.1875 to 0.1875
Outputs:
- element_power: bfloat16 [16384, 1024], P(('elem', 'chan'))
- beam_voltages: float32 [2, 64, 512], P(None, 'chan', 'elem')
Inputs may be any that keep to these rules, and one draw needn't show every extreme that they name: `subband_map`: distinct channel numbers.
All inputs are finite; a program needn't handle non-finite values.
Results may differ from a plain program's by a relative error of at most 0.007.
Values may be sent and summed in bfloat16 or wider, within the bound.
A program may use at most 128 MiB of HBM per device.

v0:
```python
import math
import jax
import jax.numpy as jnp
from jax import lax
from jax.sharding import Mesh
from jax.sharding import PartitionSpec as P

FRAMES = 4
SUB_C = 4
ELEM = ("elem_0", "elem_1", "elem_2")
ELEM_CHAN = ("elem_0", "elem_1", "elem_2", "chan")


def in_order(parts, dim):
    parts = jnp.moveaxis(parts, 0, dim)
    dims = parts.shape
    return parts.reshape(*dims[:dim], dims[dim] * dims[dim + 1], *dims[dim + 2 :])


def all_blocks(array, axes, turns):
    parts = array[None]
    for k in turns:
        parts = lax.all_gather(parts, axes[k], axis=0, tiled=True)
    held = [lax.axis_size(axes[k]) for k in reversed(turns)]
    parts = parts.reshape(*held, *array.shape)
    turned = sorted(range(len(turns)), key=lambda place: turns[len(turns) - 1 - place])
    return parts.transpose(*turned, *range(len(turns), parts.ndim)).reshape(-1, *array.shape)


def gather_axes(array, axes, turns, dim):
    return in_order(all_blocks(array, axes, turns), dim)


def filtered(voltages, delays, prototype):
    tap_count, chan_count = prototype.shape
    blocks = FRAMES + tap_count - 1
    window_len = blocks * chan_count

    def window(samples, offset):
        return lax.dynamic_slice_in_dim(samples, offset, window_len, 0)

    segments = jax.vmap(jax.vmap(window, in_axes=(0, 0)), in_axes=(0, None))(voltages, delays)
    segments = segments.reshape(voltages.shape[0], voltages.shape[1], blocks, chan_count)
    coeffs = prototype.astype(jnp.float32)
    running = jnp.zeros((voltages.shape[0], voltages.shape[1], FRAMES, chan_count), jnp.float32)
    for tap_index in range(tap_count):
        running = running + coeffs[tap_index] * segments[
            :, :, tap_index : tap_index + FRAMES, :
        ].astype(jnp.float32)
    return running.astype(jnp.bfloat16)


def spectra(filtered_wave):
    part_count, elem_count, frame_count, chan_count = filtered_wave.shape
    counter = jnp.arange(chan_count, dtype=jnp.int32)
    residue = counter[:, None] * counter[None, :] % chan_count
    radians = residue.astype(jnp.float32) * (2.0 * math.pi / chan_count)
    factor = 1.0 / math.sqrt(chan_count)
    basis = jnp.concatenate([jnp.cos(radians) * factor, jnp.sin(radians) * factor], axis=1)
    basis_high = basis.astype(jnp.bfloat16)
    basis_low = (basis - basis_high.astype(jnp.float32)).astype(jnp.bfloat16)
    flattened = filtered_wave.reshape(part_count * elem_count * frame_count, chan_count)
    product = jnp.dot(flattened, basis_high, preferred_element_type=jnp.float32)
    product = product + jnp.dot(flattened, basis_low, preferred_element_type=jnp.float32)
    product = product.reshape(part_count, elem_count, frame_count, 2, chan_count)
    spec_real = product[0, :, :, 0] + product[1, :, :, 1]
    spec_imag = product[1, :, :, 0] - product[0, :, :, 1]
    return (spec_real, spec_imag)


def beam_terms(spectra_part, weight_part):
    weight_real = weight_part[:, 0]
    weight_imag = weight_part[:, 1]

    def contract(spectral, weighting):
        return jnp.einsum("sfe,bse->sfb", spectral, weighting, preferred_element_type=jnp.float32)

    out_real = contract(spectra_part[0], weight_real) - contract(spectra_part[1], weight_imag)
    out_imag = contract(spectra_part[1], weight_real) + contract(spectra_part[0], weight_imag)
    return jnp.stack([out_real, out_imag])


def on_device(voltages, delays, prototype, subband_map, beam_weights):
    filtered_wave = filtered(voltages, delays, prototype)
    spec_real, spec_imag = spectra(filtered_wave)
    element_power = jnp.mean(spec_real * spec_real + spec_imag * spec_imag, axis=1).astype(
        jnp.bfloat16
    )
    picked = jnp.stack([spec_real[:, :, subband_map], spec_imag[:, :, subband_map]]).astype(
        jnp.bfloat16
    )
    picked = jnp.transpose(picked, (0, 3, 2, 1))
    turned = lax.all_to_all(picked, "chan", split_axis=1, concat_axis=3, tiled=True)
    local_beams = beam_weights.shape[0]
    summed = beam_terms(gather_axes(turned, ELEM, (1, 0, 2), 3), beam_weights)
    beam_voltages = summed.reshape(2, SUB_C * FRAMES, local_beams)
    return (element_power, beam_voltages)


def solution(mesh):
    finer = Mesh(
        mesh.devices.reshape(8, 2, 8, mesh.shape["chan"]), ("elem_0", "elem_1", "elem_2", "chan")
    )
    placed = (P(None, ELEM_CHAN, None), P(ELEM_CHAN), P(), P(), P(ELEM, None, "chan", None))
    return jax.shard_map(
        on_device,
        mesh=finer,
        in_specs=placed,
        out_specs=(P(ELEM_CHAN, None), P(None, "chan", ELEM)),
        check_vma=False,
    )
```

profile of v0, /device:TPU:2, one launch (start us, length us, event | category | flops | bytes accessed | tf_op | source)
XLA Modules:
  0.0 262.3 jit_solution(16402044286607184922)
XLA Ops:
  7.2 17.8 %sine_multiply_fusion = (f32[1024,1024]{1,0:T(8,128)}, f32[1024,1024]{1,0:T(8,128)}) fusion(), kind=kLoop, calls=%fused_computation.14 | loop fusion | flops 16777216 | bytes 8388608 | tf_op jit(solution)/shard_map/mul | solution.py:59
  27.1 88.3 %while.1 = (s32[]{:T(128)}, bf16[2,32,19584]{2,0,1:T(2,128)(2,1)S(1)}, s32[32,2]{0,1:T(2,128)S(1)}, bf16[32,2,19456]{2,1,0:T(2,128)(2,1)}, s32[]{:T(128)}) while((s32[]{:T(128)}, bf16[2,32,19584]{2,0,1:T(2,128)(2,1)S(1)}, s32[32,2]{0,1:T(2,128)S(1)}, bf16[32,2,19456]{2,1,0:T(2,128)(2,1)}, s32[]{:T(128)}) %tuple.51), condition=%wide.while_cond, body=%wide.while_body.sunk | while | flops 2 | bytes 157281 | solution.py:40
  27.8 2.1 bitcast_dynamic-update-slice_fusion.2
  30.5 2.1 bitcast_dynamic-update-slice_fusion.2
  33.3 2.1 bitcast_dynamic-update-slice_fusion.2
  36.0 2.1 bitcast_dynamic-update-slice_fusion.2
  38.8 2.1 bitcast_dynamic-update-slice_fusion.2
  41.5 2.1 bitcast_dynamic-update-slice_fusion.2
  44.3 2.1 bitcast_dynamic-update-slice_fusion.2
  47.1 2.1 bitcast_dynamic-update-slice_fusion.2
  49.8 2.1 bitcast_dynamic-update-slice_fusion.2
  55.3 2.1 bitcast_dynamic-update-slice_fusion.2
  58.1 2.1 bitcast_dynamic-update-slice_fusion.2
  60.8 2.1 bitcast_dynamic-update-slice_fusion.2
  63.6 2.1 bitcast_dynamic-update-slice_fusion.2
  66.4 2.1 bitcast_dynamic-update-slice_fusion.2
  69.1 2.1 bitcast_dynamic-update-slice_fusion.2
  71.9 2.1 bitcast_dynamic-update-slice_fusion.2
  74.6 2.1 bitcast_dynamic-update-slice_fusion.2
  77.4 2.1 bitcast_dynamic-update-slice_fusion.2
  80.1 2.1 bitcast_dynamic-update-slice_fusion.2
  82.9 2.1 bitcast_dynamic-update-slice_fusion.2
  85.7 2.1 bitcast_dynamic-update-slice_fusion.2
  88.4 2.1 bitcast_dynamic-update-slice_fusion.2
  91.2 2.1 bitcast_dynamic-update-slice_fusion.2
  93.9 2.1 bitcast_dynamic-update-slice_fusion.2
  96.7 2.1 bitcast_dynamic-update-slice_fusion.2
  99.5 2.1 bitcast_dynamic-update-slice_fusion.2
  102.2 2.1 bitcast_dynamic-update-slice_fusion.2
  105.0 2.1 bitcast_dynamic-update-slice_fusion.2
  107.7 2.1 bitcast_dynamic-update-slice_fusion.2
  113.2 2.1 bitcast_dynamic-update-slice_fusion.2
  115.3 3.6 %copy.41 = bf16[2,32,19456]{2,1,0:T(8,128)(2,1)} copy(bf16[2,32,19456]{2,0,1:T(2,128)(2,1)} %bitcast.82) | data formatting | bytes 4980736 | tf_op jit(solution)/shard_map/vmap(vmap())/gather | solution.py:40
  119.0 3.3 %reshape.48 = bf16[2,32,19,1024]{3,2,1,0:T(8,128)(2,1)S(1)} reshape(bf16[2,32,19456]{2,1,0:T(8,128)(2,1)} %copy.41) | data formatting | bytes 4980736 | tf_op jit(solution)/shard_map/reshape | solution.py:43
  122.3 5.1 %add_convert_fusion = bf16[2,32,4,1024]{3,2,1,0:T(4,128)(2,1)} fusion(bf16[2,32,19,1024]{3,2,1,0:T(8,128)(2,1)S(1)} %reshape.48, f32[1024]{0:T(1024)S(1)} %bitcast.102, f32[1024]{0:T(1024)S(1)} %bitcast.101, f32[1024]{0:T(1024)S(1)} %bitcast.100, f32[1024]{0:T(1024)S(1)} %bitcast.99, f32[1024]{0:T(1024)S(1)} %bitcast.98, f32[1024]{0:T(1024)S(1)} %bitcast.97, ...), kind=kLoop, calls=%fused_computation.26 | loop fusion | flops 12582912 | bytes 8978432 | tf_op jit(solution)/shard_map/convert_element_type | solution.py:50
  128.6 4.8 %fusion.1 = f32[256,2048]{1,0:T(8,128)S(1)} fusion(bf16[256,1024]{1,0:T(8,128)(2,1)S(1)} %reshape.49, f32[1024,1024]{1,0:T(8,128)} %get-tuple-element.61, f32[1024,1024]{1,0:T(8,128)} %get-tuple-element.62), kind=kOutput, calls=%fused_computation.10 | convolution fusion | flops 1082130432 | bytes 11010048 | tf_op jit(solution)/shard_map/dot_general | solution.py:63
  135.8 2.8 %reshape.50 = f32[2,32,4,2,1024]{4,3,2,1,0:T(2,128)} reshape(f32[256,2048]{1,0:T(8,128)S(1)} %fusion.10) | data formatting | bytes 4194304 | tf_op jit(solution)/shard_map/reshape | solution.py:65
  138.6 5.4 %fusion.17 = (f32[1,32,4,1,1024]{4,3,2,1,0:T(1,128)S(1)}, f32[1,32,4,1,1024]{4,3,2,1,0:T(1,128)S(1)}, f32[1,32,4,1,1024]{4,3,2,1,0:T(1,128)}, f32[1,32,4,1,1024]{4,3,2,1,0:T(1,128)}) fusion(f32[2,32,4,2,1024]{4,3,2,1,0:T(2,128)} %reshape.50), kind=kLoop, calls=%fused_computation.44 | loop fusion | bytes 4194304 | tf_op jit(solution)/shard_map/slice | solution.py:67
  144.0 2.7 %copy.58 = f32[1,32,4,1,1024]{1,2,4,3,0:T(4,128)S(1)} copy(f32[1,32,4,1,1024]{4,3,2,1,0:T(1,128)} %get-tuple-element.40) | data formatting | bytes 1048576
  146.7 3.3 %copy.59 = f32[1,32,4,1,1024]{1,2,4,3,0:T(4,128)} copy(f32[1,32,4,1,1024]{4,3,2,1,0:T(1,128)} %get-tuple-element.39) | data formatting | bytes 1048576
  150.1 2.4 copy.60
  152.5 2.4 copy.61
  154.9 5.7 %add_reduce_fusion = (f32[32,1024]{0,1:T(8,128)S(1)}, bf16[32,4,1024]{0,1,2:T(4,128)(2,1)}, bf16[32,4,1024]{0,1,2:T(4,128)(2,1)}) fusion(f32[1,32,4,1,1024]{1,2,4,3,0:T(4,128)S(1)} %copy.58, f32[1,32,4,1,1024]{1,2,4,3,0:T(4,128)} %copy.59, f32[1,32,4,1,1024]{1,2,4,3,0:T(4,128)} %copy.60, f32[1,32,4,1,1024]{1,2,4,3,0:T(4,128)} %copy.61), kind=kLoop, calls=%fused_computation.21 | loop fusion | flops 1015808 | bytes 2752512 | tf_op jit(solution)/shard_map/reduce_sum | solution.py:86
  164.9 3.4 %all-to-all-start = ((bf16[4,2,512]{2,1,0:T(2,128)(2,1)}), bf16[4,2,512]{2,1,0:T(2,128)(2,1)S(1)}, u32[]{:S(2)}, u32[]{:S(2)}) async-start(bf16[4,2,512]{2,1,0:T(2,128)(2,1)} %reshape.92), calls=%async_computation | async-start | bytes 16384 | tf_op jit(solution)/shard_map/all_to_all | solution.py:93
  169.1 4.5 %all-to-all-done = bf16[4,2,512]{2,1,0:T(2,128)(2,1)S(1)} async-done(((bf16[4,2,512]{2,1,0:T(2,128)(2,1)}), bf16[4,2,512]{2,1,0:T(2,128)(2,1)S(1)}, u32[]{:S(2)}, u32[]{:S(2)}) %all-to-all-start) | async-done | bytes 8224 | tf_op jit(solution)/shard_map/all_to_all | solution.py:93
  173.9 8.0 %all_gather.9 = bf16[2,2,4,4,128]{4,3,2,1,0:T(4,128)(2,1)S(1)} all-gather(bf16[1,2,4,4,128]{4,3,2,1,0:T(4,128)(2,1)S(1)} %broadcast_in_dim.14), channel_id=1, replica_groups=mesh['elem_0'=8,'elem_1'=2,'elem_2'=8,'chan'=4] {'elem_1'}, dimensions={0}, use_global_device_ids=true | all-gather | bytes 24576 | tf_op jit(solution)/shard_map/all_gather | solution.py:23
  181.9 29.3 %all_gather.10 = bf16[16,2,4,4,128]{4,3,2,1,0:T(4,128)(2,1)} all-gather(bf16[2,2,4,4,128]{4,3,2,1,0:T(4,128)(2,1)S(1)} %all_gather.9), channel_id=1, replica_groups=mesh['elem_0'=8,'elem_1'=2,'elem_2'=8,'chan'=4] {'elem_0'}, dimensions={0}, use_global_device_ids=true | all-gather | bytes 147456 | tf_op jit(solution)/shard_map/all_gather | solution.py:23
  212.7 36.1 %all-gather.2.cloned.1.call-done = bf16[128,2,4,4,128]{4,3,2,1,0:T(4,128)(2,1)} async-done(((bf16[16,2,4,4,128]{4,3,2,1,0:T(4,128)(2,1)}), bf16[128,2,4,4,128]{4,3,2,1,0:T(4,128)(2,1)}) %all-gather.2.cloned.1.call-update) | async-done | bytes 1048592 | tf_op jit(solution)/shard_map/all_gather | solution.py:23
  (113 shorter events, 44.1 us)
Async XLA Ops:
  7.2 17.8 %copy-start.3 = (bf16[16,1024]{1,0:T(8,128)(2,1)S(1)}, bf16[16,1024]{1,0:T(8,128)(2,1)}, u32[]{:S(2)}) copy-start(bf16[16,1024]{1,0:T(8,128)(2,1)} %param.7) | copy-start | bytes 98308
  7.2 17.9 %copy-start.2 = (bf16[2,32,19584]{2,1,0:T(8,128)(2,1)S(1)}, bf16[2,32,19584]{2,1,0:T(8,128)(2,1)}, u32[]{:S(2)}) copy-start(bf16[2,32,19584]{2,1,0:T(8,128)(2,1)} %param.5) | copy-start | bytes 7520260
  25.0 2.0 copy-start.4
  128.6 4.9 %copy-start = (f32[1024,1024]{1,0:T(8,128)S(1)}, f32[1024,1024]{1,0:T(8,128)}, u32[]{:S(2)}) copy-start(f32[1024,1024]{1,0:T(8,128)} %get-tuple-element.61) | copy-start | bytes 12582916
  128.6 5.9 %copy-start.1 = (f32[1024,1024]{1,0:T(8,128)S(1)}, f32[1024,1024]{1,0:T(8,128)}, u32[]{:S(2)}) copy-start(f32[1024,1024]{1,0:T(8,128)} %get-tuple-element.62) | copy-start | bytes 12582916
  146.7 8.2 %copy-start.5 = (s32[16]{0:T(128)S(1)}, s32[16]{0:T(128)}, u32[]{:S(2)}) copy-start(s32[16]{0:T(128)} %param.8) | copy-start | bytes 196
  164.9 8.7 %all-to-all-start = ((bf16[4,2,512]{2,1,0:T(2,128)(2,1)}), bf16[4,2,512]{2,1,0:T(2,128)(2,1)S(1)}, u32[]{:S(2)}, u32[]{:S(2)}) async-start(bf16[4,2,512]{2,1,0:T(2,128)(2,1)} %reshape.92), calls=%async_computation | async-start | bytes 16384 | tf_op jit(solution)/shard_map/all_to_all | solution.py:93
  168.3 80.5 %all-gather.2.cloned.1.call-start = ((), (), s32[]{:S(2)}) async-start(), calls=%async_computation.1 | async-start | bytes 1179648 | tf_op jit(solution)/shard_map/all_gather | solution.py:23
Sparse Core Ops, SparseCore 0:
  211.3 37.5 all-gather.1
where the time goes:
time: 263 us; the launch traced here: 262 us
  local copies, waits for them, and re-layouts  128 us (49%)
  waiting for transfers between devices  40.6 us (15%)
  blocking collectives  37.3 us (14%)
  other arithmetic  29.3 us (11%)
  between operations  14.3 us (5%)
  matrix products  9.47 us (4%)
  starting transfers between devices  3.4 us (1%)
    gather x96, local copies, waits for them, and re-layouts  88.2 us
    all_gather x2, blocking collectives, all_blocks(): parts = lax.all_gather(parts, axes[k], axis=0, tiled=True)  37.3 us
    all_gather x1, waiting for transfers between devices, all_blocks(): parts = lax.all_gather(parts, axes[k], axis=0, tiled=True)  36.1 us
    mul x1, other arithmetic, spectra(): jnp.sin(radians) * factor  17.8 us
    unnamed x21, local copies, waits for them, and re-layouts  15.4 us
    reduce_sum x1, other arithmetic, on_device(): jnp.mean(spec_real * spec_real + spec_imag * spec_imag, axis=1)  5.69 us
    slice x1, local copies, waits for them, and re-layouts, spectra(): spec_imag = product[1, :, :, 0] - product[0, :, :, 1]  5.37 us
  transfers between devices with their start and end apart: 2, of which 2 were waited for; matrix products, arithmetic and copies ran while one was open for 1% of the time, Pallas kernels for 0%

commit v1 on v0

--- a/solution.py
+++ b/solution.py
@@ -20,7 +20,16 @@
 def all_blocks(array, axes, turns):
     parts = array[None]
     for k in turns:
-        parts = lax.all_gather(parts, axes[k], axis=0, tiled=True)
+        incoming_x = axes[k]
+        parts = jnp.concatenate(
+            lax.all_to_all(
+                jnp.stack([parts] * lax.psum(1, axis_name=incoming_x)),
+                axis_name=incoming_x,
+                split_axis=0,
+                concat_axis=0,
+            ),
+            0,
+        )
     held = [lax.axis_size(axes[k]) for k in reversed(turns)]
     parts = parts.reshape(*held, *array.shape)
     turned = sorted(range(len(turns)), key=lambda place: turns[len(turns) - 1 - place])

time: 263 us -> 235 us (0.89)
  the two profiles are of different devices: /device:TPU:2 before, /device:TPU:8 now
where the time goes in v1:
time: 235 us; the launch traced here: 233 us
  local copies, waits for them, and re-layouts  127 us (54%)
  waiting for transfers between devices  32.7 us (14%)
  other arithmetic  29.3 us (12%)
  starting transfers between devices  17.9 us (8%)
  blocking collectives  15.6 us (7%)
  matrix products  9.47 us (4%)
    gather x96, local copies, waits for them, and re-layouts  88.2 us
    all_to_all x2, waiting for transfers between devices, all_blocks(): lax.all_to_all(jnp.stack([parts] * lax.psum(1, axis_name=incoming_x)), ax...  32.7 us
    all_to_all x2, starting transfers between devices, all_blocks(): lax.all_to_all(jnp.stack([parts] * lax.psum(1, axis_name=incoming_x)), ax...  17.9 us
    mul x1, other arithmetic, spectra(): jnp.sin(radians) * factor  17.8 us
    unnamed x23, local copies, waits for them, and re-layouts  14.8 us
    all_to_all x1, blocking collectives, on_device(): lax.all_to_all(picked, 'chan', split_axis=1, concat_axis=3, tiled=True)  9.41 us
    all_to_all x1, blocking collectives, all_blocks(): lax.all_to_all(jnp.stack([parts] * lax.psum(1, axis_name=incoming_x)), ax...  6.2 us
    reduce_sum x1, other arithmetic, on_device(): jnp.mean(spec_real * spec_real + spec_imag * spec_imag, axis=1)  5.69 us
  transfers between devices with their start and end apart: 2, of which 2 were waited for; matrix products, arithmetic and copies ran while one was open for 0% of the time, Pallas kernels for 0%

profile of v1, /device:TPU:8, one launch (start us, length us, event | category | flops | bytes accessed | tf_op | source)
XLA Modules:
  0.0 233.3 jit_solution(12180305149648651257)
XLA Ops:
  0.7 17.8 %sine_multiply_fusion = (f32[1024,1024]{1,0:T(8,128)}, f32[1024,1024]{1,0:T(8,128)}) fusion(), kind=kLoop, calls=%fused_computation.14 | loop fusion | flops 16777216 | bytes 8388608 | tf_op jit(solution)/shard_map/mul | solution.py:68
  20.6 88.3 %while.1 = (s32[]{:T(128)}, bf16[2,32,19584]{2,0,1:T(2,128)(2,1)S(1)}, s32[32,2]{0,1:T(2,128)S(1)}, bf16[32,2,19456]{2,1,0:T(2,128)(2,1)}, s32[]{:T(128)}) while((s32[]{:T(128)}, bf16[2,32,19584]{2,0,1:T(2,128)(2,1)S(1)}, s32[32,2]{0,1:T(2,128)S(1)}, bf16[32,2,19456]{2,1,0:T(2,128)(2,1)}, s32[]{:T(128)}) %tuple.52), condition=%wide.while_cond, body=%wide.while_body.sunk | while | flops 2 | bytes 157281 | solution.py:49
  21.2 2.1 bitcast_dynamic-update-slice_fusion.2
  24.0 2.1 bitcast_dynamic-update-slice_fusion.2
  29.5 2.1 bitcast_dynamic-update-slice_fusion.2
  32.2 2.1 bitcast_dynamic-update-slice_fusion.2
  35.0 2.1 bitcast_dynamic-update-slice_fusion.2
  37.7 2.1 bitcast_dynamic-update-slice_fusion.2
  40.5 2.1 bitcast_dynamic-update-slice_fusion.2
  43.3 2.1 bitcast_dynamic-update-slice_fusion.2
  48.8 2.1 bitcast_dynamic-update-slice_fusion.2
  51.6 2.1 bitcast_dynamic-update-slice_fusion.2
  54.3 2.1 bitcast_dynamic-update-slice_fusion.2
  57.1 2.1 bitcast_dynamic-update-slice_fusion.2
  59.8 2.1 bitcast_dynamic-update-slice_fusion.2
  62.6 2.1 bitcast_dynamic-update-slice_fusion.2
  65.3 2.1 bitcast_dynamic-update-slice_fusion.2
  68.1 2.1 bitcast_dynamic-update-slice_fusion.2
  70.8 2.1 bitcast_dynamic-update-slice_fusion.2
  73.6 2.1 bitcast_dynamic-update-slice_fusion.2
  76.4 2.1 bitcast_dynamic-update-slice_fusion.2
  79.1 2.1 bitcast_dynamic-update-slice_fusion.2
  81.9 2.1 bitcast_dynamic-update-slice_fusion.2
  84.6 2.1 bitcast_dynamic-update-slice_fusion.2
  87.4 2.1 bitcast_dynamic-update-slice_fusion.2
  90.2 2.1 bitcast_dynamic-update-slice_fusion.2
  92.9 2.1 bitcast_dynamic-update-slice_fusion.2
  95.7 2.1 bitcast_dynamic-update-slice_fusion.2
  98.4 2.1 bitcast_dynamic-update-slice_fusion.2
  101.2 2.1 bitcast_dynamic-update-slice_fusion.2
  106.7 2.1 bitcast_dynamic-update-slice_fusion.2
  108.8 3.6 %copy.43 = bf16[2,32,19456]{2,1,0:T(8,128)(2,1)} copy(bf16[2,32,19456]{2,0,1:T(2,128)(2,1)} %bitcast.84) | data formatting | bytes 4980736 | tf_op jit(solution)/shard_map/vmap(vmap())/gather | solution.py:49
  112.5 3.3 %reshape.49 = bf16[2,32,19,1024]{3,2,1,0:T(8,128)(2,1)S(1)} reshape(bf16[2,32,19456]{2,1,0:T(8,128)(2,1)} %copy.43) | data formatting | bytes 4980736 | tf_op jit(solution)/shard_map/reshape | solution.py:52
  115.8 5.1 %add_convert_fusion = bf16[2,32,4,1024]{3,2,1,0:T(4,128)(2,1)} fusion(bf16[2,32,19,1024]{3,2,1,0:T(8,128)(2,1)S(1)} %reshape.49, f32[1024]{0:T(1024)S(1)} %bitcast.106, f32[1024]{0:T(1024)S(1)} %bitcast.105, f32[1024]{0:T(1024)S(1)} %bitcast.104, f32[1024]{0:T(1024)S(1)} %bitcast.103, f32[1024]{0:T(1024)S(1)} %bitcast.102, f32[1024]{0:T(1024)S(1)} %bitcast.101, ...), kind=kLoop, calls=%fused_computation.26 | loop fusion | flops 12582912 | bytes 8978432 | tf_op jit(solution)/shard_map/convert_element_type | solution.py:59
  122.1 4.8 %fusion.1 = f32[256,2048]{1,0:T(8,128)S(1)} fusion(bf16[256,1024]{1,0:T(8,128)(2,1)S(1)} %reshape.50, f32[1024,1024]{1,0:T(8,128)} %get-tuple-element.63, f32[1024,1024]{1,0:T(8,128)} %get-tuple-element.64), kind=kOutput, calls=%fused_computation.10 | convolution fusion | flops 1082130432 | bytes 11010048 | tf_op jit(solution)/shard_map/dot_general | solution.py:72
  129.3 2.8 %reshape.51 = f32[2,32,4,2,1024]{4,3,2,1,0:T(2,128)} reshape(f32[256,2048]{1,0:T(8,128)S(1)} %fusion.10) | data formatting | bytes 4194304 | tf_op jit(solution)/shard_map/reshape | solution.py:74
  132.1 5.4 %fusion.17 = (f32[1,32,4,1,1024]{4,3,2,1,0:T(1,128)S(1)}, f32[1,32,4,1,1024]{4,3,2,1,0:T(1,128)S(1)}, f32[1,32,4,1,1024]{4,3,2,1,0:T(1,128)}, f32[1,32,4,1,1024]{4,3,2,1,0:T(1,128)}) fusion(f32[2,32,4,2,1024]{4,3,2,1,0:T(2,128)} %reshape.51), kind=kLoop, calls=%fused_computation.45 | loop fusion | bytes 4194304 | tf_op jit(solution)/shard_map/slice | solution.py:76
  137.5 2.7 %copy.61 = f32[1,32,4,1,1024]{1,2,4,3,0:T(4,128)S(1)} copy(f32[1,32,4,1,1024]{4,3,2,1,0:T(1,128)} %get-tuple-element.42) | data formatting | bytes 1048576
  140.2 3.3 %copy.62 = f32[1,32,4,1,1024]{1,2,4,3,0:T(4,128)} copy(f32[1,32,4,1,1024]{4,3,2,1,0:T(1,128)} %get-tuple-element.41) | data formatting | bytes 1048576
  143.5 2.4 %copy.63 = f32[1,32,4,1,1024]{1,2,4,3,0:T(4,128)} copy(f32[1,32,4,1,1024]{4,3,2,1,0:T(1,128)S(1)} %get-tuple-element.40) | data formatting | bytes 1048576
  145.9 2.4 %copy.64 = f32[1,32,4,1,1024]{1,2,4,3,0:T(4,128)} copy(f32[1,32,4,1,1024]{4,3,2,1,0:T(1,128)S(1)} %get-tuple-element.39) | data formatting | bytes 1048576
  148.4 5.7 %add_reduce_fusion = (f32[32,1024]{0,1:T(8,128)S(1)}, bf16[32,4,1024]{0,1,2:T(4,128)(2,1)}, bf16[32,4,1024]{0,1,2:T(4,128)(2,1)}) fusion(f32[1,32,4,1,1024]{1,2,4,3,0:T(4,128)S(1)} %copy.61, f32[1,32,4,1,1024]{1,2,4,3,0:T(4,128)} %copy.62, f32[1,32,4,1,1024]{1,2,4,3,0:T(4,128)} %copy.63, f32[1,32,4,1,1024]{1,2,4,3,0:T(4,128)} %copy.64), kind=kLoop, calls=%fused_computation.21 | loop fusion | flops 1015808 | bytes 2752512 | tf_op jit(solution)/shard_map/reduce_sum | solution.py:95
  157.9 9.4 %all_to_all.30 = bf16[4,2,512]{2,1,0:T(2,128)(2,1)S(1)} all-to-all(bf16[4,2,512]{2,1,0:T(2,128)(2,1)S(1)} %reshape.92), channel_id=1, replica_groups=mesh['elem_0'=8,'elem_1'=2,'elem_2'=8,'chan'=4] {'chan'}, dimensions={0} | all-to-all | bytes 16384 | tf_op jit(solution)/shard_map/all_to_all | solution.py:102
  167.6 6.2 %all_to_all.31 = bf16[2,1,2,4,4,128]{5,4,3,2,1,0:T(4,128)(2,1)S(1)} all-to-all(bf16[2,1,2,4,4,128]{5,4,3,2,1,0:T(4,128)(2,1)S(1)} %pad_maximum_fusion.1), channel_id=1, replica_groups=mesh['elem_0'=8,'elem_1'=2,'elem_2'=8,'chan'=4] {'elem_1'}, dimensions={0} | all-to-all | bytes 32768 | tf_op jit(solution)/shard_map/all_to_all | solution.py:25
  174.5 10.3 %all-to-all-start.2 = ((bf16[8,2,2,4,4,128]{5,1,4,3,2,0:T(2,128)(2,1)}), bf16[8,2,2,4,4,128]{5,1,4,3,2,0:T(2,128)(2,1)S(1)}, u32[]{:S(2)}, u32[]{:S(2)}) async-start(bf16[8,2,2,4,4,128]{5,1,4,3,2,0:T(2,128)(2,1)} %stack.34), calls=%async_computation.2 | async-start | bytes 262144 | tf_op jit(solution)/shard_map/all_to_all | solution.py:25
  185.6 8.3 %all-to-all-done.2 = bf16[8,2,2,4,4,128]{5,1,4,3,2,0:T(2,128)(2,1)S(1)} async-done(((bf16[8,2,2,4,4,128]{5,1,4,3,2,0:T(2,128)(2,1)}), bf16[8,2,2,4,4,128]{5,1,4,3,2,0:T(2,128)(2,1)S(1)}, u32[]{:S(2)}, u32[]{:S(2)}) %all-to-all-start.2) | async-done | bytes 131104 | tf_op jit(solution)/shard_map/all_to_all | solution.py:25
  195.2 7.5 %all-to-all-start.3 = ((bf16[8,16,2,4,4,128]{5,1,4,3,2,0:T(8,128)(2,1)}), bf16[8,16,2,4,4,128]{5,1,4,3,2,0:T(8,128)(2,1)S(1)}, u32[]{:S(2)}, u32[]{:S(2)}) async-start(bf16[8,16,2,4,4,128]{5,1,4,3,2,0:T(8,128)(2,1)} %stack.35), calls=%async_computation.3 | async-start | bytes 2097152 | tf_op jit(solution)/shard_map/all_to_all | solution.py:25
  203.1 24.4 %all-to-all-done.3 = bf16[8,16,2,4,4,128]{5,1,4,3,2,0:T(8,128)(2,1)S(1)} async-done(((bf16[8,16,2,4,4,128]{5,1,4,3,2,0:T(8,128)(2,1)}), bf16[8,16,2,4,4,128]{5,1,4,3,2,0:T(8,128)(2,1)S(1)}, u32[]{:S(2)}, u32[]{:S(2)}) %all-to-all-start.3) | async-done | bytes 1048608 | tf_op jit(solution)/shard_map/all_to_all | solution.py:25
  (118 shorter events, 45.7 us)
Async XLA Ops:
  0.6 17.8 %copy-start.4 = (bf16[16,1024]{1,0:T(8,128)(2,1)S(1)}, bf16[16,1024]{1,0:T(8,128)(2,1)}, u32[]{:S(2)}) copy-start(bf16[16,1024]{1,0:T(8,128)(2,1)} %param.7) | copy-start | bytes 98308
  0.7 17.9 %copy-start.2 = (bf16[2,32,19584]{2,1,0:T(8,128)(2,1)S(1)}, bf16[2,32,19584]{2,1,0:T(8,128)(2,1)}, u32[]{:S(2)}) copy-start(bf16[2,32,19584]{2,1,0:T(8,128)(2,1)} %param.5) | copy-start | bytes 7520260
  18.5 2.0 copy-start.5
  122.0 4.9 %copy-start = (f32[1024,1024]{1,0:T(8,128)S(1)}, f32[1024,1024]{1,0:T(8,128)}, u32[]{:S(2)}) copy-start(f32[1024,1024]{1,0:T(8,128)} %get-tuple-element.63) | copy-start | bytes 12582916
  122.0 5.9 %copy-start.1 = (f32[1024,1024]{1,0:T(8,128)S(1)}, f32[1024,1024]{1,0:T(8,128)}, u32[]{:S(2)}) copy-start(f32[1024,1024]{1,0:T(8,128)} %get-tuple-element.64) | copy-start | bytes 12582916
  140.2 8.2 %copy-start.6 = (s32[16]{0:T(128)S(1)}, s32[16]{0:T(128)}, u32[]{:S(2)}) copy-start(s32[16]{0:T(128)} %param.8) | copy-start | bytes 196
  154.1 48.7 %copy-start.3 = (bf16[4,2,4,16384]{3,2,1,0:T(4,128)(2,1)S(1)}, bf16[4,2,4,16384]{3,2,1,0:T(4,128)(2,1)}, u32[]{:S(2)}) copy-start(bf16[4,2,4,16384]{3,2,1,0:T(4,128)(2,1)} %param.9) | copy-start | bytes 3145732
  174.5 19.4 %all-to-all-start.2 = ((bf16[8,2,2,4,4,128]{5,1,4,3,2,0:T(2,128)(2,1)}), bf16[8,2,2,4,4,128]{5,1,4,3,2,0:T(2,128)(2,1)S(1)}, u32[]{:S(2)}, u32[]{:S(2)}) async-start(bf16[8,2,2,4,4,128]{5,1,4,3,2,0:T(2,128)(2,1)} %stack.34), calls=%async_computation.2 | async-start | bytes 262144 | tf_op jit(solution)/shard_map/all_to_all | solution.py:25
  195.2 32.3 %all-to-all-start.3 = ((bf16[8,16,2,4,4,128]{5,1,4,3,2,0:T(8,128)(2,1)}), bf16[8,16,2,4,4,128]{5,1,4,3,2,0:T(8,128)(2,1)S(1)}, u32[]{:S(2)}, u32[]{:S(2)}) async-start(bf16[8,16,2,4,4,128]{5,1,4,3,2,0:T(8,128)(2,1)} %stack.35), calls=%async_computation.3 | async-start | bytes 2097152 | tf_op jit(solution)/shard_map/all_to_all | solution.py:25
